TPU v7x, 32 devices: a whole 2x2x4 slice. The times are simulated.
32 devices in a mesh: row: 2 (over x), col: 16 (over z, y, core).
Axes of the slice: x: 2, y: 2, z: 4, core: 2. Of those that a mesh axis runs over, the one named last changes fastest.
Arguments:
- eigvecs: float32 [16384, 4096], P('row', 'col'), may hold values from -6 to 6
- v_panels: float32 [8, 16384, 256], P(None, 'row', 'col'), as said below
- t_panels: float32 [8, 256, 256], P(None, None, 'col'), as said below
Outputs:
- rotated: float32 [16384, 4096], P('row', 'col')
Inputs may be any that keep to these rules, and one draw needn't show every extreme that they name: `v_panels`: in panel k, vector j is zero in rows above k * 256 + j + 1, equals 1 in that row and is dense below it. t_panels[k] is upper triangular and V_k t_panels[k] V_k^T = I minus the product of the panel's 256 Householder reflections, each I - 2 v v^T / (v^T v), taken in the order of j; its diagonal lies in (0, 2].
All inputs are finite; a program needn't handle non-finite values.
Results may differ from a plain program's by a relative error of at most 0.00015.
Values sent between devices are 32-bit elements; how exact they have to be, the bound alone decides.
A program may use at most 192 MiB of HBM per device.

v0:
```python
import jax
import jax.numpy as jnp
from jax import lax
from jax.sharding import PartitionSpec as P

exact_precision = lax.Precision.HIGHEST


def matmul(left, right):
    return jnp.dot(left, right, preferred_element_type=jnp.float32, precision=exact_precision)


def project(left, right):
    return lax.dot_general(
        left,
        right,
        (((0,), (0,)), ((), ())),
        precision=exact_precision,
        preferred_element_type=jnp.float32,
    )


def local(eigvecs, v_panels, t_panels):
    panels_total = v_panels.shape[0]
    every_v, every_t = (
        lax.all_gather(v_panels, "col", axis=2, tiled=True),
        lax.all_gather(t_panels, "col", axis=2, tiled=True),
    )
    current = eigvecs
    for panel_index in reversed(range(panels_total)):
        vectors = every_v[panel_index]
        factor = every_t[panel_index]
        projected = lax.psum(project(vectors, current), "row")
        current = current - matmul(vectors, matmul(factor, projected))
    return current


def solution(mesh):
    in_specs = (P("row", "col"), P(None, "row", "col"), P(None, None, "col"))
    out_specs = P("row", "col")
    return jax.shard_map(local, mesh=mesh, in_specs=in_specs, out_specs=out_specs, check_vma=False)
```

profile of v0, /device:TPU:0, one launch (start us, length us, event | category | flops | bytes accessed | tf_op | source)
XLA Modules:
  0.0 791.7 jit_solution(15002217065631639125)
XLA Ops:
  8.1 329.7 %all-gather.3.cloned.1.call-done = f32[8,8192,256]{1,2,0:T(8,128)} async-done(((f32[8,8192,16]{1,2,0:T(8,128)}), f32[8,8192,256]{1,2,0:T(8,128)}) %all-gather.3.cloned.1.call-update) | async-done | bytes 67108880 | tf_op jit(solution)/shard_map/all_gather | solution.py:26
  337.7 11.4 %fusion.8 = f32[256,256]{1,0:T(8,128)} fusion(f32[8192,256]{1,0:T(8,128)} %param.3, f32[8,8192,256]{1,2,0:T(8,128)} %all-gather.3.cloned.1.call-done), kind=kOutput, calls=%fused_computation.24 | convolution fusion | flops 6442450944 | bytes 17039360 | tf_op jit(solution)/shard_map/dot_general | solution.py:14
  358.4 23.0 %all-gather.5.cloned.1.call-done = f32[8,256,256]{1,2,0:T(8,128)} async-done(((f32[8,256,16]{1,2,0:T(8,128)}), f32[8,256,256]{1,2,0:T(8,128)}) %all-gather.5.cloned.1.call-update) | async-done | bytes 2097168 | tf_op jit(solution)/shard_map/all_gather | solution.py:27
  381.4 24.3 %all-reduce.9.cloned.1.call-done = f32[256,256]{1,0:T(8,128)} async-done(((f32[256,256]{1,0:T(8,128)}), f32[256,256]{1,0:T(8,128)}) %all-reduce.9.cloned.1.call-update) | async-done | bytes 262160 | tf_op jit(solution)/shard_map/psum | solution.py:33
  407.4 11.9 %fusion.7 = f32[8192,256]{0,1:T(8,128)S(1)} fusion(f32[8192,256]{0,1:T(8,128)} %copy.4, f32[256,256]{1,0:T(8,128)S(1)} %fusion.30, f32[8,8192,256]{1,2,0:T(8,128)} %all-gather.3.cloned.1.call-done), kind=kOutput, calls=%fused_computation.15 | convolution fusion | flops 6444548096 | bytes 25427968 | tf_op jit(solution)/shard_map/dot_general | solution.py:10
  422.7 10.3 %fusion.22 = f32[256,256]{0,1:T(8,128)} fusion(f32[8192,256]{0,1:T(8,128)S(1)} %fusion.7, f32[8,8192,256]{1,2,0:T(8,128)} %all-gather.3.cloned.1.call-done), kind=kOutput, calls=%fused_computation.38 | convolution fusion | flops 6442450944 | bytes 17039360 | tf_op jit(solution)/shard_map/dot_general | solution.py:14
  433.3 23.1 %all-reduce.11.cloned.1.call-done = f32[256,256]{0,1:T(8,128)} async-done(((f32[256,256]{0,1:T(8,128)}), f32[256,256]{0,1:T(8,128)}) %all-reduce.11.cloned.1.call-update) | async-done | bytes 262160 | tf_op jit(solution)/shard_map/psum | solution.py:33
  457.8 11.9 %fusion.6 = f32[8192,256]{0,1:T(8,128)S(1)} fusion(f32[8192,256]{0,1:T(8,128)} %copy-done, f32[256,256]{1,0:T(8,128)S(1)} %fusion.29, f32[8,8192,256]{1,2,0:T(8,128)} %all-gather.3.cloned.1.call-done), kind=kOutput, calls=%fused_computation.13 | convolution fusion | flops 6444548096 | bytes 25427968 | tf_op jit(solution)/shard_map/dot_general | solution.py:10
  473.1 10.1 %fusion.21 = f32[256,256]{0,1:T(8,128)} fusion(f32[8192,256]{0,1:T(8,128)S(1)} %fusion.6, f32[8,8192,256]{1,2,0:T(8,128)} %all-gather.3.cloned.1.call-done), kind=kOutput, calls=%fused_computation.37 | convolution fusion | flops 6442450944 | bytes 17039360 | tf_op jit(solution)/shard_map/dot_general | solution.py:14
  483.9 22.8 %all-reduce.13.cloned.1.call-done = f32[256,256]{0,1:T(8,128)} async-done(((f32[256,256]{0,1:T(8,128)}), f32[256,256]{0,1:T(8,128)}) %all-reduce.13.cloned.1.call-update) | async-done | bytes 262160 | tf_op jit(solution)/shard_map/psum | solution.py:33
  508.0 11.9 %fusion.5 = f32[8192,256]{0,1:T(8,128)S(1)} fusion(f32[8192,256]{0,1:T(8,128)} %copy-done.1, f32[256,256]{1,0:T(8,128)S(1)} %fusion.28, f32[8,8192,256]{1,2,0:T(8,128)} %all-gather.3.cloned.1.call-done), kind=kOutput, calls=%fused_computation.11 | convolution fusion | flops 6444548096 | bytes 25427968 | tf_op jit(solution)/shard_map/dot_general | solution.py:10
  523.3 10.1 %fusion.20 = f32[256,256]{0,1:T(8,128)} fusion(f32[8192,256]{0,1:T(8,128)S(1)} %fusion.5, f32[8,8192,256]{1,2,0:T(8,128)} %all-gather.3.cloned.1.call-done), kind=kOutput, calls=%fused_computation.36 | convolution fusion | flops 6442450944 | bytes 17039360 | tf_op jit(solution)/shard_map/dot_general | solution.py:14
  533.7 23.2 %all-reduce.15.cloned.1.call-done = f32[256,256]{0,1:T(8,128)} async-done(((f32[256,256]{0,1:T(8,128)}), f32[256,256]{0,1:T(8,128)}) %all-reduce.15.cloned.1.call-update) | async-done | bytes 262160 | tf_op jit(solution)/shard_map/psum | solution.py:33
  558.3 11.9 %fusion.4 = f32[8192,256]{0,1:T(8,128)S(1)} fusion(f32[8192,256]{0,1:T(8,128)} %copy-done.2, f32[256,256]{1,0:T(8,128)S(1)} %fusion.27, f32[8,8192,256]{1,2,0:T(8,128)} %all-gather.3.cloned.1.call-done), kind=kOutput, calls=%fused_computation.9 | convolution fusion | flops 6444548096 | bytes 25427968 | tf_op jit(solution)/shard_map/dot_general | solution.py:10
  584.0 23.2 %all-reduce.17.cloned.1.call-done = f32[256,256]{0,1:T(8,128)} async-done(((f32[256,256]{0,1:T(8,128)}), f32[256,256]{0,1:T(8,128)}) %all-reduce.17.cloned.1.call-update) | async-done | bytes 262160 | tf_op jit(solution)/shard_map/psum | solution.py:33
  608.5 11.9 %fusion.3 = f32[8192,256]{0,1:T(8,128)S(1)} fusion(f32[8192,256]{0,1:T(8,128)} %copy-done.3, f32[256,256]{1,0:T(8,128)S(1)} %fusion.26, f32[8,8192,256]{1,2,0:T(8,128)} %all-gather.3.cloned.1.call-done), kind=kOutput, calls=%fused_computation.7 | convolution fusion | flops 6444548096 | bytes 25427968 | tf_op jit(solution)/shard_map/dot_general | solution.py:10
  623.8 10.1 %fusion.18 = f32[256,256]{0,1:T(8,128)} fusion(f32[8192,256]{0,1:T(8,128)S(1)} %fusion.3, f32[8,8192,256]{1,2,0:T(8,128)} %all-gather.3.cloned.1.call-done), kind=kOutput, calls=%fused_computation.34 | convolution fusion | flops 6442450944 | bytes 17039360 | tf_op jit(solution)/shard_map/dot_general | solution.py:14
  634.3 23.2 %all-reduce.19.cloned.1.call-done = f32[256,256]{0,1:T(8,128)} async-done(((f32[256,256]{0,1:T(8,128)}), f32[256,256]{0,1:T(8,128)}) %all-reduce.19.cloned.1.call-update) | async-done | bytes 262160 | tf_op jit(solution)/shard_map/psum | solution.py:33
  658.8 11.9 %fusion.2 = f32[8192,256]{0,1:T(8,128)S(1)} fusion(f32[8192,256]{0,1:T(8,128)} %copy-done.4, f32[256,256]{1,0:T(8,128)S(1)} %fusion.25, f32[8,8192,256]{1,2,0:T(8,128)} %all-gather.3.cloned.1.call-done), kind=kOutput, calls=%fused_computation.5 | convolution fusion | flops 6444548096 | bytes 25427968 | tf_op jit(solution)/shard_map/dot_general | solution.py:10
  674.1 10.1 %fusion.17 = f32[256,256]{0,1:T(8,128)} fusion(f32[8192,256]{0,1:T(8,128)S(1)} %fusion.2, f32[8,8192,256]{1,2,0:T(8,128)} %all-gather.3.cloned.1.call-done), kind=kOutput, calls=%fused_computation.33 | convolution fusion | flops 6442450944 | bytes 17039360 | tf_op jit(solution)/shard_map/dot_general | solution.py:14
  684.7 22.9 %all-reduce.21.cloned.1.call-done = f32[256,256]{0,1:T(8,128)} async-done(((f32[256,256]{0,1:T(8,128)}), f32[256,256]{0,1:T(8,128)}) %all-reduce.21.cloned.1.call-update) | async-done | bytes 262160 | tf_op jit(solution)/shard_map/psum | solution.py:33
  709.0 11.9 %fusion.1 = f32[8192,256]{0,1:T(8,128)S(1)} fusion(f32[8192,256]{0,1:T(8,128)} %copy-done.5, f32[256,256]{1,0:T(8,128)S(1)} %fusion.24, f32[8,8192,256]{1,2,0:T(8,128)} %all-gather.3.cloned.1.call-done), kind=kOutput, calls=%fused_computation.3 | convolution fusion | flops 6444548096 | bytes 25427968 | tf_op jit(solution)/shard_map/dot_general | solution.py:10
  734.5 23.5 %all-reduce.23.cloned.1.call-done = f32[256,256]{0,1:T(8,128)} async-done(((f32[256,256]{0,1:T(8,128)}), f32[256,256]{0,1:T(8,128)}) %all-reduce.23.cloned.1.call-update) | async-done | bytes 262160 | tf_op jit(solution)/shard_map/psum | solution.py:33
  759.3 16.4 %fusion = f32[8192,256]{0,1:T(8,128)} fusion(f32[8192,256]{0,1:T(8,128)} %copy-done.6, f32[256,256]{1,0:T(8,128)S(1)} %fusion.23, f32[8,8192,256]{1,2,0:T(8,128)} %all-gather.3.cloned.1.call-done), kind=kOutput, calls=%fused_computation.1 | convolution fusion | flops 6444548096 | bytes 25427968 | tf_op jit(solution)/shard_map/dot_general | solution.py:10
  (48 shorter events, 77.0 us)
Async XLA Ops:
  6.5 331.2 %all-gather.3.cloned.1.call-start = ((), (), s32[]{:S(2)}) async-start(), calls=%async_computation | async-start | bytes 71303168 | tf_op jit(solution)/shard_map/all_gather | solution.py:26
  7.3 374.2 %all-gather.5.cloned.1.call-start = ((), (), s32[]{:S(2)}) async-start(), calls=%async_computation.2 | async-start | bytes 2228224 | tf_op jit(solution)/shard_map/all_gather | solution.py:27
  8.0 397.7 %all-reduce.9.cloned.1.call-start = ((), (), s32[]{:S(2)}) async-start(), calls=%async_computation.1 | async-start | bytes 524288 | tf_op jit(solution)/shard_map/psum | solution.py:33
  349.1 107.3 %all-reduce.11.cloned.1.call-start = ((), (), s32[]{:S(2)}) async-start(), calls=%async_computation.3 | async-start | bytes 524288 | tf_op jit(solution)/shard_map/psum | solution.py:33
  419.3 3.4 copy-start
  422.7 33.8 %copy-start.7 = (f32[8,256,256]{1,2,0:T(8,128)S(1)}, f32[8,256,256]{1,2,0:T(8,128)}, u32[]{:S(2)}) copy-start(f32[8,256,256]{1,2,0:T(8,128)} %all-gather.5.cloned.1.call-done) | copy-start | bytes 6291460
  433.0 73.7 %all-reduce.13.cloned.1.call-start = ((), (), s32[]{:S(2)}) async-start(), calls=%async_computation.4 | async-start | bytes 524288 | tf_op jit(solution)/shard_map/psum | solution.py:33
  469.7 3.4 copy-start.1
  483.2 73.7 %all-reduce.15.cloned.1.call-start = ((), (), s32[]{:S(2)}) async-start(), calls=%async_computation.5 | async-start | bytes 524288 | tf_op jit(solution)/shard_map/psum | solution.py:33
  519.9 3.4 copy-start.2
  533.5 73.7 %all-reduce.17.cloned.1.call-start = ((), (), s32[]{:S(2)}) async-start(), calls=%async_computation.6 | async-start | bytes 524288 | tf_op jit(solution)/shard_map/psum | solution.py:33
  570.2 3.4 copy-start.3
  583.7 73.7 %all-reduce.19.cloned.1.call-start = ((), (), s32[]{:S(2)}) async-start(), calls=%async_computation.7 | async-start | bytes 524288 | tf_op jit(solution)/shard_map/psum | solution.py:33
  620.4 3.4 copy-start.4
  634.0 73.7 %all-reduce.21.cloned.1.call-start = ((), (), s32[]{:S(2)}) async-start(), calls=%async_computation.8 | async-start | bytes 524288 | tf_op jit(solution)/shard_map/psum | solution.py:33
  670.7 3.4 copy-start.5
  684.2 73.7 %all-reduce.23.cloned.1.call-start = ((), (), s32[]{:S(2)}) async-start(), calls=%async_computation.9 | async-start | bytes 524288 | tf_op jit(solution)/shard_map/psum | solution.py:33
  720.9 3.4 copy-start.6
Sparse Core Ops, SparseCore 0:
  8.9 328.7 all-gather.2
  339.9 41.4 all-gather.4
  383.7 22.0 all-reduce.8
  433.1 23.2 all-reduce.10
  483.3 23.2 all-reduce.12
  533.6 23.2 all-reduce.14
  583.8 23.2 all-reduce.16
  634.1 23.2 all-reduce.18
  684.3 23.2 all-reduce.20
  734.6 23.2 all-reduce.22
where the time goes:
time: 796 us; the launch traced here: 792 us
  waiting for transfers between devices  540 us (68%)
  matrix products  193 us (24%)
  local copies, waits for them, and re-layouts  41.6 us (5%)
  between operations  13.9 us (2%)
    all_gather x1, waiting for transfers between devices, local(): lax.all_gather(v_panels, 'col', axis=2, tiled=True)  330 us
    psum x8, waiting for transfers between devices, local(): projected = lax.psum(project(vectors, current), 'row')  186 us
    dot_general x16, matrix products, matmul(): jnp.dot(left, right, preferred_element_type=jnp.float32, precision=exact_...  111 us
    dot_general x8, matrix products, project(): lax.dot_general(left, right, (((0,), (0,)), ((), ())), precision=exact_pr...  82.4 us
    unnamed x17, local copies, waits for them, and re-layouts  32.7 us
    all_gather x1, waiting for transfers between devices, local(): lax.all_gather(t_panels, 'col', axis=2, tiled=True)  23 us
  transfers between devices with their start and end apart: 10, of which 10 were waited for; matrix products, arithmetic and copies ran while one was open for 3% of the time, Pallas kernels for 0%

commit v1 on v0

--- a/solution.py
+++ b/solution.py
@@ -30,7 +30,9 @@
     for panel_index in reversed(range(panels_total)):
         vectors = every_v[panel_index]
         factor = every_t[panel_index]
-        projected = lax.psum(project(vectors, current), "row")
+        part = project(vectors, current)
+        terms = lax.all_gather(part, "row")
+        projected = jnp.sum(terms, axis=0)
         current = current - matmul(vectors, matmul(factor, projected))
     return current
 

time: 796 us -> 661 us (0.83)
  waiting for transfers between devices: 540 us -> 345 us
  blocking collectives: 0 us -> 64.3 us
  local copies, waits for them, and re-layouts: 41.6 us -> 20.3 us
  matrix products: 193 us -> 208 us
    psum x8 -> x0, waiting for transfers between devices: 186 us -> none  [local(): projected = lax.psum(project(vectors, current), 'row')]
    all_gather x0 -> x8, blocking collectives: none -> 64.3 us  [local(): terms = lax.all_gather(part, 'row')]
    unnamed x17 -> x15, local copies, waits for them, and re-layouts: 32.7 us -> 8.95 us
    dot_general x8, matrix products: 82.4 us -> 98 us  [project(): lax.dot_general(left, right, (((0,), (0,)), ((), ())), precision=exact_pr...]
    all_gather x1, waiting for transfers between devices: 330 us -> 321 us  [local(): lax.all_gather(v_panels, 'col', axis=2, tiled=True)]
  transfers between devices with their start and end apart: 10 -> 2, of which waited for: 10 -> 2; matrix products, arithmetic and copies ran while one was open for 3% -> 3% of each run, Pallas kernels for 0% -> 0%
where the time goes in v1:
time: 661 us; the launch traced here: 657 us
  waiting for transfers between devices  345 us (52%)
  matrix products  208 us (31%)
  blocking collectives  64.3 us (10%)
  local copies, waits for them, and re-layouts  20.3 us (3%)
  between operations  14.3 us (2%)
    all_gather x1, waiting for transfers between devices, local(): lax.all_gather(v_panels, 'col', axis=2, tiled=True)  321 us
    dot_general x16, matrix products, matmul(): jnp.dot(left, right, preferred_element_type=jnp.float32, precision=exact_...  110 us
    dot_general x8, matrix products, project(): lax.dot_general(left, right, (((0,), (0,)), ((), ())), precision=exact_pr...  98 us
    all_gather x8, blocking collectives, local(): terms = lax.all_gather(part, 'row')  64.3 us
    all_gather x1, waiting for transfers between devices, local(): lax.all_gather(t_panels, 'col', axis=2, tiled=True)  23.3 us
  transfers between devices with their start and end apart: 2, of which 2 were waited for; matrix products, arithmetic and copies ran while one was open for 3% of the time, Pallas kernels for 0%

profile of v1, /device:TPU:0, one launch (start us, length us, event | category | flops | bytes accessed | tf_op | source)
XLA Modules:
  0.0 657.1 jit_solution(12147726348671748409)
XLA Ops:
  8.0 8.9 %copy.6 = f32[8192,256]{0,1:T(8,128)} copy(f32[8192,256]{1,0:T(8,128)} %param.3) | data formatting | bytes 16777216 | tf_op args[0]
  16.9 320.8 %all-gather.11.cloned.1.call-done = f32[8,8192,256]{1,2,0:T(8,128)} async-done(((f32[8,8192,16]{1,2,0:T(8,128)}), f32[8,8192,256]{1,2,0:T(8,128)}) %all-gather.11.cloned.1.call-update) | async-done | bytes 67108880 | tf_op jit(solution)/shard_map/all_gather | solution.py:26
  337.7 10.7 %fusion.8 = f32[256,256]{1,0:T(8,128)S(1)} fusion(f32[8192,256]{1,0:T(8,128)} %param.3, f32[8,8192,256]{1,2,0:T(8,128)} %all-gather.11.cloned.1.call-done), kind=kOutput, calls=%fused_computation.24 | convolution fusion | flops 6442450944 | bytes 17039360 | tf_op jit(solution)/shard_map/dot_general | solution.py:14
  348.4 9.6 %all-gather = f32[512,256]{1,0:T(8,128)S(1)} all-gather(f32[256,256]{1,0:T(8,128)S(1)} %fusion.8), channel_id=2, replica_groups=mesh['row'=2,'col'=16] {'row'}, dimensions={0}, use_global_device_ids=true | all-gather | bytes 786432 | tf_op jit(solution)/shard_map/all_gather | solution.py:34
  358.1 23.3 %all-gather.13.cloned.1.call-done = f32[8,256,256]{1,2,0:T(8,128)} async-done(((f32[8,256,16]{1,2,0:T(8,128)}), f32[8,256,256]{1,2,0:T(8,128)}) %all-gather.13.cloned.1.call-update) | async-done | bytes 2097168 | tf_op jit(solution)/shard_map/all_gather | solution.py:27
  383.0 11.9 %fusion.7 = f32[8192,256]{0,1:T(8,128)S(1)} fusion(f32[8192,256]{0,1:T(8,128)} %copy.6, f32[256,256]{1,0:T(8,128)S(1)} %fusion.30, f32[8,8192,256]{1,2,0:T(8,128)} %all-gather.11.cloned.1.call-done), kind=kOutput, calls=%fused_computation.15 | convolution fusion | flops 6444548096 | bytes 25427968 | tf_op jit(solution)/shard_map/dot_general | solution.py:10
  394.9 12.5 %fusion.22 = f32[256,256]{0,1:T(8,128)S(1)} fusion(f32[8192,256]{0,1:T(8,128)S(1)} %fusion.7, f32[8,8192,256]{1,2,0:T(8,128)} %all-gather.11.cloned.1.call-done), kind=kOutput, calls=%fused_computation.38 | convolution fusion | flops 6442450944 | bytes 17039360 | tf_op jit(solution)/shard_map/dot_general | solution.py:14
  407.4 9.3 %all-gather.1 = f32[512,256]{0,1:T(8,128)S(1)} all-gather(f32[256,256]{0,1:T(8,128)S(1)} %fusion.22), channel_id=3, replica_groups=mesh['row'=2,'col'=16] {'row'}, dimensions={0}, use_global_device_ids=true | all-gather | bytes 786432 | tf_op jit(solution)/shard_map/all_gather | solution.py:34
  418.9 11.9 %fusion.6 = f32[8192,256]{0,1:T(8,128)S(1)} fusion(f32[8192,256]{0,1:T(8,128)} %copy-done.1, f32[256,256]{1,0:T(8,128)S(1)} %fusion.29, f32[8,8192,256]{1,2,0:T(8,128)} %all-gather.11.cloned.1.call-done), kind=kOutput, calls=%fused_computation.13 | convolution fusion | flops 6444548096 | bytes 25427968 | tf_op jit(solution)/shard_map/dot_general | solution.py:10
  430.9 12.5 %fusion.21 = f32[256,256]{0,1:T(8,128)S(1)} fusion(f32[8192,256]{0,1:T(8,128)S(1)} %fusion.6, f32[8,8192,256]{1,2,0:T(8,128)} %all-gather.11.cloned.1.call-done), kind=kOutput, calls=%fused_computation.37 | convolution fusion | flops 6442450944 | bytes 17039360 | tf_op jit(solution)/shard_map/dot_general | solution.py:14
  443.3 8.5 %all-gather.2 = f32[512,256]{0,1:T(8,128)S(1)} all-gather(f32[256,256]{0,1:T(8,128)S(1)} %fusion.21), channel_id=4, replica_groups=mesh['row'=2,'col'=16] {'row'}, dimensions={0}, use_global_device_ids=true | all-gather | bytes 786432 | tf_op jit(solution)/shard_map/all_gather | solution.py:34
  454.1 11.9 %fusion.5 = f32[8192,256]{0,1:T(8,128)S(1)} fusion(f32[8192,256]{0,1:T(8,128)} %copy-done.2, f32[256,256]{1,0:T(8,128)S(1)} %fusion.28, f32[8,8192,256]{1,2,0:T(8,128)} %all-gather.11.cloned.1.call-done), kind=kOutput, calls=%fused_computation.11 | convolution fusion | flops 6444548096 | bytes 25427968 | tf_op jit(solution)/shard_map/dot_general | solution.py:10
  466.0 12.5 %fusion.20 = f32[256,256]{0,1:T(8,128)S(1)} fusion(f32[8192,256]{0,1:T(8,128)S(1)} %fusion.5, f32[8,8192,256]{1,2,0:T(8,128)} %all-gather.11.cloned.1.call-done), kind=kOutput, calls=%fused_computation.36 | convolution fusion | flops 6442450944 | bytes 17039360 | tf_op jit(solution)/shard_map/dot_general | solution.py:14
  478.5 7.8 %all-gather.3 = f32[512,256]{0,1:T(8,128)S(1)} all-gather(f32[256,256]{0,1:T(8,128)S(1)} %fusion.20), channel_id=5, replica_groups=mesh['row'=2,'col'=16] {'row'}, dimensions={0}, use_global_device_ids=true | all-gather | bytes 786432 | tf_op jit(solution)/shard_map/all_gather | solution.py:34
  488.6 11.9 %fusion.4 = f32[8192,256]{0,1:T(8,128)S(1)} fusion(f32[8192,256]{0,1:T(8,128)} %copy-done.3, f32[256,256]{1,0:T(8,128)S(1)} %fusion.27, f32[8,8192,256]{1,2,0:T(8,128)} %all-gather.11.cloned.1.call-done), kind=kOutput, calls=%fused_computation.9 | convolution fusion | flops 6444548096 | bytes 25427968 | tf_op jit(solution)/shard_map/dot_general | solution.py:10
  500.5 12.5 %fusion.19 = f32[256,256]{0,1:T(8,128)S(1)} fusion(f32[8192,256]{0,1:T(8,128)S(1)} %fusion.4, f32[8,8192,256]{1,2,0:T(8,128)} %all-gather.11.cloned.1.call-done), kind=kOutput, calls=%fused_computation.35 | convolution fusion | flops 6442450944 | bytes 17039360 | tf_op jit(solution)/shard_map/dot_general | solution.py:14
  522.5 11.9 %fusion.3 = f32[8192,256]{0,1:T(8,128)S(1)} fusion(f32[8192,256]{0,1:T(8,128)} %copy-done.4, f32[256,256]{1,0:T(8,128)S(1)} %fusion.26, f32[8,8192,256]{1,2,0:T(8,128)} %all-gather.11.cloned.1.call-done), kind=kOutput, calls=%fused_computation.7 | convolution fusion | flops 6444548096 | bytes 25427968 | tf_op jit(solution)/shard_map/dot_general | solution.py:10
  534.5 12.5 %fusion.18 = f32[256,256]{0,1:T(8,128)S(1)} fusion(f32[8192,256]{0,1:T(8,128)S(1)} %fusion.3, f32[8,8192,256]{1,2,0:T(8,128)} %all-gather.11.cloned.1.call-done), kind=kOutput, calls=%fused_computation.34 | convolution fusion | flops 6442450944 | bytes 17039360 | tf_op jit(solution)/shard_map/dot_general | solution.py:14
  556.5 11.9 %fusion.2 = f32[8192,256]{0,1:T(8,128)S(1)} fusion(f32[8192,256]{0,1:T(8,128)} %copy-done.5, f32[256,256]{1,0:T(8,128)S(1)} %fusion.25, f32[8,8192,256]{1,2,0:T(8,128)} %all-gather.11.cloned.1.call-done), kind=kOutput, calls=%fused_computation.5 | convolution fusion | flops 6444548096 | bytes 25427968 | tf_op jit(solution)/shard_map/dot_general | solution.py:10
  568.4 12.5 %fusion.17 = f32[256,256]{0,1:T(8,128)S(1)} fusion(f32[8192,256]{0,1:T(8,128)S(1)} %fusion.2, f32[8,8192,256]{1,2,0:T(8,128)} %all-gather.11.cloned.1.call-done), kind=kOutput, calls=%fused_computation.33 | convolution fusion | flops 6442450944 | bytes 17039360 | tf_op jit(solution)/shard_map/dot_general | solution.py:14
  590.5 11.9 %fusion.1 = f32[8192,256]{0,1:T(8,128)S(1)} fusion(f32[8192,256]{0,1:T(8,128)} %copy-done.6, f32[256,256]{1,0:T(8,128)S(1)} %fusion.24, f32[8,8192,256]{1,2,0:T(8,128)} %all-gather.11.cloned.1.call-done), kind=kOutput, calls=%fused_computation.3 | convolution fusion | flops 6444548096 | bytes 25427968 | tf_op jit(solution)/shard_map/dot_general | solution.py:10
  602.4 12.5 %fusion.16 = f32[256,256]{0,1:T(8,128)S(1)} fusion(f32[8192,256]{0,1:T(8,128)S(1)} %fusion.1, f32[8,8192,256]{1,2,0:T(8,128)} %all-gather.11.cloned.1.call-done), kind=kOutput, calls=%fused_computation.32 | convolution fusion | flops 6442450944 | bytes 17039360 | tf_op jit(solution)/shard_map/dot_general | solution.py:14
  624.5 16.2 %fusion = f32[8192,256]{0,1:T(8,128)} fusion(f32[8192,256]{0,1:T(8,128)} %copy-done, f32[256,256]{1,0:T(8,128)S(1)} %fusion.23, f32[8,8192,256]{1,2,0:T(8,128)} %all-gather.11.cloned.1.call-done), kind=kOutput, calls=%fused_computation.1 | convolution fusion | flops 6444548096 | bytes 25427968 | tf_op jit(solution)/shard_map/dot_general | solution.py:10
  640.7 9.0 %copy.7 = f32[8192,256]{1,0:T(8,128)} copy(f32[8192,256]{0,1:T(8,128)} %fusion) | data formatting | bytes 16777216 | tf_op jit(solution)/shard_map/sub | solution.py:36
  (45 shorter events, 48.1 us)
Async XLA Ops:
  6.5 331.2 %all-gather.11.cloned.1.call-start = ((), (), s32[]{:S(2)}) async-start(), calls=%async_computation | async-start | bytes 71303168 | tf_op jit(solution)/shard_map/all_gather | solution.py:26
  7.3 374.2 %all-gather.13.cloned.1.call-start = ((), (), s32[]{:S(2)}) async-start(), calls=%async_computation.1 | async-start | bytes 2228224 | tf_op jit(solution)/shard_map/all_gather | solution.py:27
  394.9 12.5 %copy-start.1 = (f32[8192,256]{0,1:T(8,128)}, f32[8192,256]{0,1:T(8,128)S(1)}, u32[]{:S(2)}) copy-start(f32[8192,256]{0,1:T(8,128)S(1)} %fusion.7) | copy-start | bytes 25165828
  430.9 12.5 %copy-start.2 = (f32[8192,256]{0,1:T(8,128)}, f32[8192,256]{0,1:T(8,128)S(1)}, u32[]{:S(2)}) copy-start(f32[8192,256]{0,1:T(8,128)S(1)} %fusion.6) | copy-start | bytes 25165828
  466.0 12.5 %copy-start.3 = (f32[8192,256]{0,1:T(8,128)}, f32[8192,256]{0,1:T(8,128)S(1)}, u32[]{:S(2)}) copy-start(f32[8192,256]{0,1:T(8,128)S(1)} %fusion.5) | copy-start | bytes 25165828
  500.5 12.5 %copy-start.4 = (f32[8192,256]{0,1:T(8,128)}, f32[8192,256]{0,1:T(8,128)S(1)}, u32[]{:S(2)}) copy-start(f32[8192,256]{0,1:T(8,128)S(1)} %fusion.4) | copy-start | bytes 25165828
  534.4 12.5 %copy-start.5 = (f32[8192,256]{0,1:T(8,128)}, f32[8192,256]{0,1:T(8,128)S(1)}, u32[]{:S(2)}) copy-start(f32[8192,256]{0,1:T(8,128)S(1)} %fusion.3) | copy-start | bytes 25165828
  568.4 12.5 %copy-start.6 = (f32[8192,256]{0,1:T(8,128)}, f32[8192,256]{0,1:T(8,128)S(1)}, u32[]{:S(2)}) copy-start(f32[8192,256]{0,1:T(8,128)S(1)} %fusion.2) | copy-start | bytes 25165828
  602.4 12.5 %copy-start = (f32[8192,256]{0,1:T(8,128)}, f32[8192,256]{0,1:T(8,128)S(1)}, u32[]{:S(2)}) copy-start(f32[8192,256]{0,1:T(8,128)S(1)} %fusion.1) | copy-start | bytes 25165828
Sparse Core Ops, SparseCore 0:
  8.9 328.7 all-gather.10
  339.9 41.4 all-gather.12
